TPU v7x, 32 devices: a whole 2x2x4 slice. The times are simulated.
32 devices in a mesh: gx: 2 (over core), gy: 4 (over y, x), gz: 4 (over z).
Axes of the slice: x: 2, y: 2, z: 4, core: 2. Of those that a mesh axis runs over, the one named last changes fastest.
Arguments:
- permanent_field: float32 [12, 24, 24, 3], P('gx', 'gy', 'gz'), may hold values from -6 to 6
- polar: float32 [12, 24, 24], P('gx', 'gy', 'gz'), may hold values from 0.4 to 1.4
- jitter: float32 [12, 24, 24, 3], P('gx', 'gy', 'gz'), may hold values from -0.2 to 0.2
- neighbors: int32 [12, 24, 24, 56], P('gx', 'gy', 'gz'), may hold values from -1 to 987, as said below
Outputs:
- dipoles: float32 [12, 24, 24, 3], P('gx', 'gy', 'gz')
- residual: float32 [12, 24, 24, 3], P('gx', 'gy', 'gz')
- step_lengths: float32 [8], replicated
Inputs may be any that keep to these rules, and one draw needn't show every extreme that they name: `neighbors`: each entry is -1 or the flat index of a neighbour in the device's block extended by two sites on every side, with an offset d of squared length 1 to 5 (each component -2 to 2), each offset at most once in a row; the -1 entries come after all others; if site j stands in site i's row with offset d then i stands in j's row with offset -d, the box being periodic.
All inputs are finite; a program needn't handle non-finite values.
Results may differ from a plain program's by a relative error of at most 0.0003.
Values sent between devices are 32-bit elements.
A program may use at most 64 MiB of HBM per device.

v0:
```python
import jax
import jax.numpy as jnp
from jax import lax
from jax.sharding import PartitionSpec as P

ITERS = 8


thole_damping = 0.39
site_spacing = 3.5


def padded_2(cells, sides, width, closed):
    for axis, dim in sides:
        count = lax.axis_size(axis)
        ends = count if closed else count - 1
        head = lax.slice_in_dim(cells, 0, width, axis=dim)
        tail = lax.slice_in_dim(cells, cells.shape[dim] - width, cells.shape[dim], axis=dim)
        cells = jnp.concatenate(
            [
                lax.ppermute(tail, axis, [(i, (i + 1) % count) for i in range(ends)]),
                cells,
                lax.ppermute(head, axis, [((i + 1) % count, i) for i in range(ends)]),
            ],
            axis=dim,
        )
    return cells


def geometry(offsets, jit_self, jit_other, pol_self, pol_other, present):
    separation = (offsets + jit_other - jit_self) * site_spacing
    separation = jnp.where(present[..., None], separation, site_spacing)
    dist_sq = jnp.sum(separation * separation, axis=-1)
    distance = jnp.sqrt(dist_sq)
    dist_cube = dist_sq * distance
    damping = thole_damping * dist_cube / jnp.sqrt(pol_self * pol_other)
    falloff = jnp.exp(-damping)
    lam_three = 1.0 - falloff
    lam_five = 1.0 - (1.0 + damping) * falloff
    isotropic = jnp.where(present, lam_three / dist_cube, 0.0)
    radial = jnp.where(present, 3.0 * lam_five / (dist_cube * dist_sq), 0.0)
    return (separation, isotropic, radial)


def couple(separation, isotropic, radial, values):
    projection = jnp.sum(separation * values, axis=-1, keepdims=True)
    return jnp.sum(
        radial[..., None] * projection * separation - isotropic[..., None] * values, axis=-2
    )


def local(permanent_field, polar, jitter, neighbors):
    cell_edge = polar.shape[0]
    padded_edge = cell_edge + 4
    padded_count = padded_edge * padded_edge * padded_edge
    site_count = cell_edge * cell_edge * cell_edge
    slots = neighbors.shape[-1]
    bundle = jnp.concatenate([jitter, polar[..., None]], axis=-1)
    padded = padded_2(bundle, (("gx", 0), ("gy", 1), ("gz", 2)), 2, True)
    flattened = padded.reshape(padded_count, 4)
    neighbor_rows = neighbors.reshape(site_count, slots)
    present = neighbor_rows >= 0
    clipped = jnp.where(present, neighbor_rows, 0)
    plane_a = clipped // (padded_edge * padded_edge)
    plane_b = clipped // padded_edge % padded_edge
    plane_c = clipped % padded_edge
    site_index = lax.broadcasted_iota(jnp.int32, (site_count, 1), 0)
    home_x = site_index // (cell_edge * cell_edge)
    home_y = site_index // cell_edge % cell_edge
    home_z = site_index % cell_edge
    offsets = jnp.stack(
        [plane_a - 2 - home_x, plane_b - 2 - home_y, plane_c - 2 - home_z], axis=-1
    ).astype(jnp.float32)
    remote = flattened[clipped]
    weights = polar.reshape(site_count, 1)
    separation, isotropic, radial = geometry(
        offsets, jitter.reshape(site_count, 1, 3), remote[..., :3], weights, remote[..., 3], present
    )

    def operate(vector):
        ghosts = padded_2(
            vector.reshape(cell_edge, cell_edge, cell_edge, 3),
            (("gx", 0), ("gy", 1), ("gz", 2)),
            2,
            True,
        )
        values = ghosts.reshape(padded_count, 3)[clipped]
        return vector / weights - couple(separation, isotropic, radial, values)

    source = permanent_field.reshape(site_count, 3)
    dipoles = weights * source
    residual = source - operate(dipoles)
    lengths = []

    def joined(left_vec, right_vec, other_vec):
        return lax.psum(
            (jnp.sum(left_vec * right_vec), jnp.sum(right_vec * other_vec)), ("gx", "gy", "gz")
        )

    scaled = weights * residual
    image = operate(scaled)
    gamma_now, delta_now = joined(residual, scaled, image)
    step_len = gamma_now / delta_now
    direction = scaled
    image_dir = image
    for number in range(ITERS):
        lengths.append(step_len)
        dipoles = dipoles + step_len * direction
        residual = residual - step_len * image_dir
        if number + 1 < ITERS:
            scaled = weights * residual
            image = operate(scaled)
            gamma_next, delta_now = joined(residual, scaled, image)
            beta_now = gamma_next / gamma_now
            step_len = gamma_next / (delta_now - beta_now * gamma_next / step_len)
            direction = scaled + beta_now * direction
            image_dir = image + beta_now * image_dir
            gamma_now = gamma_next
    shape_out = (cell_edge, cell_edge, cell_edge, 3)
    return (
        dipoles.reshape(shape_out),
        residual.reshape(shape_out),
        jnp.stack(lengths).astype(jnp.float32),
    )


def solution(mesh):
    return jax.shard_map(
        local,
        mesh=mesh,
        in_specs=(
            P("gx", "gy", "gz", None),
            P("gx", "gy", "gz"),
            P("gx", "gy", "gz", None),
            P("gx", "gy", "gz", None),
        ),
        out_specs=(P("gx", "gy", "gz", None), P("gx", "gy", "gz", None), P()),
        check_vma=False,
    )
```

profile of v0, /device:TPU:0, one launch (start us, length us, event | category | flops | bytes accessed | tf_op | source)
XLA Modules:
  0.0 860.4 jit_solution(15508087018226480596)
XLA Ops:
  9.2 3.0 collective-permute-start.8
  22.6 3.7 collective-permute-start.5
  28.5 5.7 collective-permute-done.11
  34.8 23.2 %gather_fusion.1 = f32[12096,3]{1,0:T(8,128)} fusion(f32[1000,3]{1,0:T(8,128)S(1)} %copy.226, s32[12288]{0:T(1024)S(1)} %pad_clamp_fusion), kind=kCustom, calls=%fused_computation.1 | custom fusion | bytes 338688 | tf_op jit(solution)/shard_map/gather | solution.py:87
  58.0 4.9 copy.228
  63.7 23.2 %gather_fusion = f32[12096,4]{1,0:T(8,128)} fusion(f32[1000,4]{1,0:T(8,128)S(1)} %copy.218, s32[12288]{0:T(1024)S(1)} %pad_clamp_fusion), kind=kCustom, calls=%fused_computation | custom fusion | bytes 435456 | tf_op jit(solution)/shard_map/gather | solution.py:74
  86.9 7.0 slice.343
  93.9 4.9 copy.313
  98.8 4.8 copy.314
  111.5 3.3 collective-permute-start.17
  114.8 7.3 collective-permute-done.16
  124.2 23.2 %gather_fusion.2 = f32[12096,3]{1,0:T(8,128)} fusion(f32[1000,3]{1,0:T(8,128)S(1)} %copy.233, s32[12288]{0:T(1024)S(1)} %pad_clamp_fusion), kind=kCustom, calls=%fused_computation.2 | custom fusion | bytes 338688 | tf_op jit(solution)/shard_map/gather | solution.py:87
  147.5 4.8 copy.235
  153.2 40.2 %all-reduce.7 = (f32[]{:T(128)}, f32[]{:T(128)}) all-reduce(f32[]{:T(128)} %get-tuple-element.30, f32[]{:T(128)} %get-tuple-element.29), channel_id=1, replica_groups=mesh['gx'=2,'gy'=4,'gz'=4] {'gx','gy','gz'}, use_global_device_ids=true, to_apply=%region_4.5 | all-reduce | flops 2 | bytes 16 | tf_op jit(solution)/shard_map/psum | solution.py:96
  203.7 3.0 collective-permute-start.23
  206.7 7.3 collective-permute-done.22
  216.1 23.2 %gather_fusion.3 = f32[12096,3]{1,0:T(8,128)} fusion(f32[1000,3]{1,0:T(8,128)S(1)} %copy.239, s32[12288]{0:T(1024)S(1)} %pad_clamp_fusion), kind=kCustom, calls=%fused_computation.3 | custom fusion | bytes 338688 | tf_op jit(solution)/shard_map/gather | solution.py:87
  239.4 4.8 copy.241
  245.2 40.0 %all-reduce.6 = (f32[]{:T(128)}, f32[]{:T(128)}) all-reduce(f32[]{:T(128)} %get-tuple-element.16, f32[]{:T(128)} %get-tuple-element.15), channel_id=1, replica_groups=mesh['gx'=2,'gy'=4,'gz'=4] {'gx','gy','gz'}, use_global_device_ids=true, to_apply=%region_10.11 | all-reduce | flops 2 | bytes 16 | tf_op jit(solution)/shard_map/psum | solution.py:96
  299.0 2.8 collective-permute-start.29
  301.8 7.2 collective-permute-done.28
  311.6 23.2 %gather_fusion.4 = f32[12096,3]{1,0:T(8,128)} fusion(f32[1000,3]{1,0:T(8,128)S(1)} %copy.245, s32[12288]{0:T(1024)S(1)} %pad_clamp_fusion), kind=kCustom, calls=%fused_computation.4 | custom fusion | bytes 338688 | tf_op jit(solution)/shard_map/gather | solution.py:87
  334.9 4.8 copy.247
  340.6 40.0 %all-reduce.5 = (f32[]{:T(128)}, f32[]{:T(128)}) all-reduce(f32[]{:T(128)} %get-tuple-element.28, f32[]{:T(128)} %get-tuple-element.27), channel_id=1, replica_groups=mesh['gx'=2,'gy'=4,'gz'=4] {'gx','gy','gz'}, use_global_device_ids=true, to_apply=%region_16.17 | all-reduce | flops 2 | bytes 16 | tf_op jit(solution)/shard_map/psum | solution.py:96
  393.8 2.8 collective-permute-start.35
  396.6 7.3 collective-permute-done.34
  406.2 23.2 %gather_fusion.5 = f32[12096,3]{1,0:T(8,128)} fusion(f32[1000,3]{1,0:T(8,128)S(1)} %copy.251, s32[12288]{0:T(1024)S(1)} %pad_clamp_fusion), kind=kCustom, calls=%fused_computation.5 | custom fusion | bytes 338688 | tf_op jit(solution)/shard_map/gather | solution.py:87
  429.5 4.8 copy.253
  435.2 40.0 %all-reduce.4 = (f32[]{:T(128)}, f32[]{:T(128)}) all-reduce(f32[]{:T(128)} %get-tuple-element.26, f32[]{:T(128)} %get-tuple-element.25), channel_id=1, replica_groups=mesh['gx'=2,'gy'=4,'gz'=4] {'gx','gy','gz'}, use_global_device_ids=true, to_apply=%region_22.23 | all-reduce | flops 2 | bytes 16 | tf_op jit(solution)/shard_map/psum | solution.py:96
  488.4 2.8 collective-permute-start.41
  491.2 7.2 collective-permute-done.40
  501.0 23.2 %gather_fusion.6 = f32[12096,3]{1,0:T(8,128)} fusion(f32[1000,3]{1,0:T(8,128)S(1)} %copy.257, s32[12288]{0:T(1024)S(1)} %pad_clamp_fusion), kind=kCustom, calls=%fused_computation.6 | custom fusion | bytes 338688 | tf_op jit(solution)/shard_map/gather | solution.py:87
  524.3 4.8 copy.259
  530.0 40.3 %all-reduce.3 = (f32[]{:T(128)}, f32[]{:T(128)}) all-reduce(f32[]{:T(128)} %get-tuple-element.24, f32[]{:T(128)} %get-tuple-element.23), channel_id=1, replica_groups=mesh['gx'=2,'gy'=4,'gz'=4] {'gx','gy','gz'}, use_global_device_ids=true, to_apply=%region_28.29 | all-reduce | flops 2 | bytes 16 | tf_op jit(solution)/shard_map/psum | solution.py:96
  583.5 2.8 collective-permute-start.47
  586.2 7.3 collective-permute-done.46
  595.9 23.2 %gather_fusion.7 = f32[12096,3]{1,0:T(8,128)} fusion(f32[1000,3]{1,0:T(8,128)S(1)} %copy.263, s32[12288]{0:T(1024)S(1)} %pad_clamp_fusion), kind=kCustom, calls=%fused_computation.7 | custom fusion | bytes 338688 | tf_op jit(solution)/shard_map/gather | solution.py:87
  619.1 4.8 copy.265
  624.8 40.0 %all-reduce.2 = (f32[]{:T(128)}, f32[]{:T(128)}) all-reduce(f32[]{:T(128)} %get-tuple-element.22, f32[]{:T(128)} %get-tuple-element.21), channel_id=1, replica_groups=mesh['gx'=2,'gy'=4,'gz'=4] {'gx','gy','gz'}, use_global_device_ids=true, to_apply=%region_34.35 | all-reduce | flops 2 | bytes 16 | tf_op jit(solution)/shard_map/psum | solution.py:96
  678.0 2.8 collective-permute-start.53
  680.8 7.2 collective-permute-done.52
  690.6 23.2 %gather_fusion.8 = f32[12096,3]{1,0:T(8,128)} fusion(f32[1000,3]{1,0:T(8,128)S(1)} %copy.269, s32[12288]{0:T(1024)S(1)} %pad_clamp_fusion), kind=kCustom, calls=%fused_computation.8 | custom fusion | bytes 338688 | tf_op jit(solution)/shard_map/gather | solution.py:87
  713.9 4.8 copy.271
  719.6 40.0 %all-reduce.1 = (f32[]{:T(128)}, f32[]{:T(128)}) all-reduce(f32[]{:T(128)} %get-tuple-element.20, f32[]{:T(128)} %get-tuple-element.19), channel_id=1, replica_groups=mesh['gx'=2,'gy'=4,'gz'=4] {'gx','gy','gz'}, use_global_device_ids=true, to_apply=%region_40.41 | all-reduce | flops 2 | bytes 16 | tf_op jit(solution)/shard_map/psum | solution.py:96
  775.7 7.3 collective-permute-done.58
  785.3 23.2 %gather_fusion.9 = f32[12096,3]{1,0:T(8,128)} fusion(f32[1000,3]{1,0:T(8,128)S(1)} %copy.275, s32[12288]{0:T(1024)S(1)} %pad_clamp_fusion), kind=kCustom, calls=%fused_computation.9 | custom fusion | bytes 338688 | tf_op jit(solution)/shard_map/gather | solution.py:87
  808.5 4.9 copy.277
  814.3 40.0 %all-reduce = (f32[]{:T(128)}, f32[]{:T(128)}) all-reduce(f32[]{:T(128)} %get-tuple-element.32, f32[]{:T(128)} %get-tuple-element.31), channel_id=1, replica_groups=mesh['gx'=2,'gy'=4,'gz'=4] {'gx','gy','gz'}, use_global_device_ids=true, to_apply=%region_46.47 | all-reduce | flops 2 | bytes 16 | tf_op jit(solution)/shard_map/psum | solution.py:96
  (282 shorter events, 125.3 us)
Async XLA Ops:
  2.7 6.4 collective-permute-start.6
  3.3 5.8 collective-permute-start.7
  4.9 8.2 collective-permute-start
  5.5 7.7 collective-permute-start.1
  9.2 7.8 collective-permute-start.8
  12.1 4.8 collective-permute-start.9
  14.0 7.3 collective-permute-start.2
  15.0 6.3 collective-permute-start.3
  17.1 11.3 %collective-permute-start.10 = (f32[10,10,2,3]{2,1,0,3:T(8,128)S(1)}, f32[10,10,2,3]{2,1,0,3:T(8,128)S(1)}, u32[]{:S(2)}, u32[]{:S(2)}) collective-permute-start(f32[10,10,2,3]{2,1,0,3:T(8,128)S(1)} %get-tuple-element.96), channel_id=1, source_target_pairs={{0,1},{1,2},{2,3},{3,0},{4,5},{5,6},{6,7},{7,4},{8,9},{9,10},{10,1... | collective-permute-start | bytes 7208 | tf_op jit(solution)/shard_map/ppermute | solution.py:21
  19.2 15.0 %collective-permute-start.11 = (f32[10,10,2,3]{2,1,0,3:T(8,128)S(1)}, f32[10,10,2,3]{2,1,0,3:T(8,128)S(1)}, u32[]{:S(2)}, u32[]{:S(2)}) collective-permute-start(f32[10,10,2,3]{2,1,0,3:T(8,128)S(1)} %get-tuple-element.97), channel_id=1, source_target_pairs={{1,0},{2,1},{3,2},{0,3},{5,4},{6,5},{7,6},{4,7},{9,8},{10,9},{11,1... | collective-permute-start | bytes 7208 | tf_op jit(solution)/shard_map/ppermute | solution.py:23
  22.4 40.5 %collective-permute-start.4 = (f32[10,10,2,4]{2,3,1,0:T(4,128)S(1)}, f32[10,10,2,4]{2,3,1,0:T(4,128)S(1)}, u32[]{:S(2)}, u32[]{:S(2)}) collective-permute-start(f32[10,10,2,4]{2,3,1,0:T(4,128)S(1)} %get-tuple-element.98), channel_id=1, source_target_pairs={{0,1},{1,2},{2,3},{3,0},{4,5},{5,6},{6,7},{7,4},{8,9},{9,10},{10,1... | collective-permute-start | bytes 9608 | tf_op jit(solution)/shard_map/ppermute | solution.py:21
  22.6 40.3 %collective-permute-start.5 = (f32[10,10,2,4]{2,3,1,0:T(4,128)S(1)}, f32[10,10,2,4]{2,3,1,0:T(4,128)S(1)}, u32[]{:S(2)}, u32[]{:S(2)}) collective-permute-start(f32[10,10,2,4]{2,3,1,0:T(4,128)S(1)} %get-tuple-element.99), channel_id=1, source_target_pairs={{1,0},{2,1},{3,2},{0,3},{5,4},{6,5},{7,6},{4,7},{9,8},{10,9},{11,1... | collective-permute-start | bytes 9608 | tf_op jit(solution)/shard_map/ppermute | solution.py:23
  105.7 4.9 collective-permute-start.14
  106.4 4.3 collective-permute-start.15
  110.9 11.1 %collective-permute-start.16 = (f32[10,10,2,3]{2,1,0,3:T(8,128)S(1)}, f32[10,10,2,3]{2,1,0,3:T(8,128)S(1)}, u32[]{:S(2)}, u32[]{:S(2)}) collective-permute-start(f32[10,10,2,3]{2,1,0,3:T(8,128)S(1)} %get-tuple-element.94), channel_id=1, source_target_pairs={{0,1},{1,2},{2,3},{3,0},{4,5},{5,6},{6,7},{7,4},{8,9},{9,10},{10,1... | collective-permute-start | bytes 7208 | tf_op jit(solution)/shard_map/ppermute | solution.py:21
  111.5 12.1 %collective-permute-start.17 = (f32[10,10,2,3]{2,1,0,3:T(8,128)S(1)}, f32[10,10,2,3]{2,1,0,3:T(8,128)S(1)}, u32[]{:S(2)}, u32[]{:S(2)}) collective-permute-start(f32[10,10,2,3]{2,1,0,3:T(8,128)S(1)} %get-tuple-element.95), channel_id=1, source_target_pairs={{1,0},{2,1},{3,2},{0,3},{5,4},{6,5},{7,6},{4,7},{9,8},{10,9},{11,1... | collective-permute-start | bytes 7208 | tf_op jit(solution)/shard_map/ppermute | solution.py:23
  195.0 1.4 collective-permute-start.19
  196.4 5.1 collective-permute-start.20
  198.8 3.9 collective-permute-start.21
  202.9 11.1 %collective-permute-start.22 = (f32[10,10,2,3]{2,1,0,3:T(8,128)S(1)}, f32[10,10,2,3]{2,1,0,3:T(8,128)S(1)}, u32[]{:S(2)}, u32[]{:S(2)}) collective-permute-start(f32[10,10,2,3]{2,1,0,3:T(8,128)S(1)} %get-tuple-element.92), channel_id=1, source_target_pairs={{0,1},{1,2},{2,3},{3,0},{4,5},{5,6},{6,7},{7,4},{8,9},{9,10},{10,1... | collective-permute-start | bytes 7208 | tf_op jit(solution)/shard_map/ppermute | solution.py:21
  203.7 11.8 %collective-permute-start.23 = (f32[10,10,2,3]{2,1,0,3:T(8,128)S(1)}, f32[10,10,2,3]{2,1,0,3:T(8,128)S(1)}, u32[]{:S(2)}, u32[]{:S(2)}) collective-permute-start(f32[10,10,2,3]{2,1,0,3:T(8,128)S(1)} %get-tuple-element.93), channel_id=1, source_target_pairs={{1,0},{2,1},{3,2},{0,3},{5,4},{6,5},{7,6},{4,7},{9,8},{10,9},{11,1... | collective-permute-start | bytes 7208 | tf_op jit(solution)/shard_map/ppermute | solution.py:23
  291.5 5.5 collective-permute-start.26
  293.9 3.9 collective-permute-start.27
  297.9 11.1 %collective-permute-start.28 = (f32[10,10,2,3]{2,1,0,3:T(8,128)S(1)}, f32[10,10,2,3]{2,1,0,3:T(8,128)S(1)}, u32[]{:S(2)}, u32[]{:S(2)}) collective-permute-start(f32[10,10,2,3]{2,1,0,3:T(8,128)S(1)} %get-tuple-element.90), channel_id=1, source_target_pairs={{0,1},{1,2},{2,3},{3,0},{4,5},{5,6},{6,7},{7,4},{8,9},{9,10},{10,1... | collective-permute-start | bytes 7208 | tf_op jit(solution)/shard_map/ppermute | solution.py:21
  299.0 12.0 %collective-permute-start.29 = (f32[10,10,2,3]{2,1,0,3:T(8,128)S(1)}, f32[10,10,2,3]{2,1,0,3:T(8,128)S(1)}, u32[]{:S(2)}, u32[]{:S(2)}) collective-permute-start(f32[10,10,2,3]{2,1,0,3:T(8,128)S(1)} %get-tuple-element.91), channel_id=1, source_target_pairs={{1,0},{2,1},{3,2},{0,3},{5,4},{6,5},{7,6},{4,7},{9,8},{10,9},{11,1... | collective-permute-start | bytes 7208 | tf_op jit(solution)/shard_map/ppermute | solution.py:23
  384.9 1.4 collective-permute-start.31
  386.3 5.3 collective-permute-start.32
  388.6 3.9 collective-permute-start.33
  392.7 11.1 %collective-permute-start.34 = (f32[10,10,2,3]{2,1,0,3:T(8,128)S(1)}, f32[10,10,2,3]{2,1,0,3:T(8,128)S(1)}, u32[]{:S(2)}, u32[]{:S(2)}) collective-permute-start(f32[10,10,2,3]{2,1,0,3:T(8,128)S(1)} %get-tuple-element.88), channel_id=1, source_target_pairs={{0,1},{1,2},{2,3},{3,0},{4,5},{5,6},{6,7},{7,4},{8,9},{9,10},{10,1... | collective-permute-start | bytes 7208 | tf_op jit(solution)/shard_map/ppermute | solution.py:21
  393.8 11.8 %collective-permute-start.35 = (f32[10,10,2,3]{2,1,0,3:T(8,128)S(1)}, f32[10,10,2,3]{2,1,0,3:T(8,128)S(1)}, u32[]{:S(2)}, u32[]{:S(2)}) collective-permute-start(f32[10,10,2,3]{2,1,0,3:T(8,128)S(1)} %get-tuple-element.89), channel_id=1, source_target_pairs={{1,0},{2,1},{3,2},{0,3},{5,4},{6,5},{7,6},{4,7},{9,8},{10,9},{11,1... | collective-permute-start | bytes 7208 | tf_op jit(solution)/shard_map/ppermute | solution.py:23
  480.9 5.5 collective-permute-start.38
  483.2 3.9 collective-permute-start.39
  487.3 11.1 %collective-permute-start.40 = (f32[10,10,2,3]{2,1,0,3:T(8,128)S(1)}, f32[10,10,2,3]{2,1,0,3:T(8,128)S(1)}, u32[]{:S(2)}, u32[]{:S(2)}) collective-permute-start(f32[10,10,2,3]{2,1,0,3:T(8,128)S(1)} %get-tuple-element.86), channel_id=1, source_target_pairs={{0,1},{1,2},{2,3},{3,0},{4,5},{5,6},{6,7},{7,4},{8,9},{9,10},{10,1... | collective-permute-start | bytes 7208 | tf_op jit(solution)/shard_map/ppermute | solution.py:21
  488.4 12.0 %collective-permute-start.41 = (f32[10,10,2,3]{2,1,0,3:T(8,128)S(1)}, f32[10,10,2,3]{2,1,0,3:T(8,128)S(1)}, u32[]{:S(2)}, u32[]{:S(2)}) collective-permute-start(f32[10,10,2,3]{2,1,0,3:T(8,128)S(1)} %get-tuple-element.87), channel_id=1, source_target_pairs={{1,0},{2,1},{3,2},{0,3},{5,4},{6,5},{7,6},{4,7},{9,8},{10,9},{11,1... | collective-permute-start | bytes 7208 | tf_op jit(solution)/shard_map/ppermute | solution.py:23
  574.5 1.4 collective-permute-start.43
  576.0 5.3 collective-permute-start.44
  578.3 3.9 collective-permute-start.45
  582.4 11.1 %collective-permute-start.46 = (f32[10,10,2,3]{2,1,0,3:T(8,128)S(1)}, f32[10,10,2,3]{2,1,0,3:T(8,128)S(1)}, u32[]{:S(2)}, u32[]{:S(2)}) collective-permute-start(f32[10,10,2,3]{2,1,0,3:T(8,128)S(1)} %get-tuple-element.84), channel_id=1, source_target_pairs={{0,1},{1,2},{2,3},{3,0},{4,5},{5,6},{6,7},{7,4},{8,9},{9,10},{10,1... | collective-permute-start | bytes 7208 | tf_op jit(solution)/shard_map/ppermute | solution.py:21
  583.5 11.8 %collective-permute-start.47 = (f32[10,10,2,3]{2,1,0,3:T(8,128)S(1)}, f32[10,10,2,3]{2,1,0,3:T(8,128)S(1)}, u32[]{:S(2)}, u32[]{:S(2)}) collective-permute-start(f32[10,10,2,3]{2,1,0,3:T(8,128)S(1)} %get-tuple-element.85), channel_id=1, source_target_pairs={{1,0},{2,1},{3,2},{0,3},{5,4},{6,5},{7,6},{4,7},{9,8},{10,9},{11,1... | collective-permute-start | bytes 7208 | tf_op jit(solution)/shard_map/ppermute | solution.py:23
  669.1 1.4 collective-permute-start.49
  670.5 5.5 collective-permute-start.50
  672.9 3.9 collective-permute-start.51
  677.0 11.1 %collective-permute-start.52 = (f32[10,10,2,3]{2,1,0,3:T(8,128)S(1)}, f32[10,10,2,3]{2,1,0,3:T(8,128)S(1)}, u32[]{:S(2)}, u32[]{:S(2)}) collective-permute-start(f32[10,10,2,3]{2,1,0,3:T(8,128)S(1)} %get-tuple-element.82), channel_id=1, source_target_pairs={{0,1},{1,2},{2,3},{3,0},{4,5},{5,6},{6,7},{7,4},{8,9},{9,10},{10,1... | collective-permute-start | bytes 7208 | tf_op jit(solution)/shard_map/ppermute | solution.py:21
  678.0 12.0 %collective-permute-start.53 = (f32[10,10,2,3]{2,1,0,3:T(8,128)S(1)}, f32[10,10,2,3]{2,1,0,3:T(8,128)S(1)}, u32[]{:S(2)}, u32[]{:S(2)}) collective-permute-start(f32[10,10,2,3]{2,1,0,3:T(8,128)S(1)} %get-tuple-element.83), channel_id=1, source_target_pairs={{1,0},{2,1},{3,2},{0,3},{5,4},{6,5},{7,6},{4,7},{9,8},{10,9},{11,1... | collective-permute-start | bytes 7208 | tf_op jit(solution)/shard_map/ppermute | solution.py:23
  765.4 5.3 collective-permute-start.56
  767.7 3.9 collective-permute-start.57
  771.8 11.1 %collective-permute-start.58 = (f32[10,10,2,3]{2,1,0,3:T(8,128)S(1)}, f32[10,10,2,3]{2,1,0,3:T(8,128)S(1)}, u32[]{:S(2)}, u32[]{:S(2)}) collective-permute-start(f32[10,10,2,3]{2,1,0,3:T(8,128)S(1)} %get-tuple-element.80), channel_id=1, source_target_pairs={{0,1},{1,2},{2,3},{3,0},{4,5},{5,6},{6,7},{7,4},{8,9},{9,10},{10,1... | collective-permute-start | bytes 7208 | tf_op jit(solution)/shard_map/ppermute | solution.py:21
  772.9 11.8 %collective-permute-start.59 = (f32[10,10,2,3]{2,1,0,3:T(8,128)S(1)}, f32[10,10,2,3]{2,1,0,3:T(8,128)S(1)}, u32[]{:S(2)}, u32[]{:S(2)}) collective-permute-start(f32[10,10,2,3]{2,1,0,3:T(8,128)S(1)} %get-tuple-element.81), channel_id=1, source_target_pairs={{1,0},{2,1},{3,2},{0,3},{5,4},{6,5},{7,6},{4,7},{9,8},{10,9},{11,1... | collective-permute-start | bytes 7208 | tf_op jit(solution)/shard_map/ppermute | solution.py:23
  (16 other events, 92.0 us)
where the time goes:
time: 862 us; the launch traced here: 860 us
  blocking collectives  321 us (37%)
  local copies, waits for them, and re-layouts  307 us (36%)
  waiting for transfers between devices  107 us (12%)
  starting transfers between devices  80.1 us (9%)
  between operations  31.3 us (4%)
  other arithmetic  14.7 us (2%)
    psum x8, blocking collectives, joined(): lax.psum((jnp.sum(left_vec * right_vec), jnp.sum(right_vec * other_vec)),...  321 us
    gather x18, local copies, waits for them, and re-layouts, operate(): values = ghosts.reshape(padded_count, 3)[clipped]  253 us
    ppermute x30, waiting for transfers between devices, padded_2(): lax.ppermute(tail, axis, [(i, (i + 1) % count) for i in range(ends)])  78.6 us
    ppermute x30, starting transfers between devices, padded_2(): lax.ppermute(head, axis, [((i + 1) % count, i) for i in range(ends)])  47.3 us
    ppermute x30, starting transfers between devices, padded_2(): lax.ppermute(tail, axis, [(i, (i + 1) % count) for i in range(ends)])  32.8 us
    ppermute x30, waiting for transfers between devices, padded_2(): lax.ppermute(head, axis, [((i + 1) % count, i) for i in range(ends)])  28.3 us
    gather x1, local copies, waits for them, and re-layouts, local(): remote = flattened[clipped]  23.2 us
  transfers between devices with their start and end apart: 60, of which 50 were waited for; matrix products, arithmetic and copies ran while one was open for 4% of the time, Pallas kernels for 0%

commit v1 on v0

v1 whole, which is shorter than its diff:
```python
import functools

import jax
import jax.numpy as jnp
from jax import lax
from jax.experimental import pallas as pl
from jax.experimental.pallas import tpu as pltpu
from jax.sharding import PartitionSpec as P

ITERS = 8
MESH = pl.DeviceIdType.MESH
thole_damping = 0.39
site_spacing = 3.5
ROWS, LANES = 8, 128


def stencil():
    return [
        (a, b, c)
        for a in range(-2, 3)
        for b in range(-2, 3)
        for c in range(-2, 3)
        if 1 <= a * a + b * b + c * c <= 5
    ]


def roll(value, shift):
    shift = shift % LANES
    return value if shift == 0 else pltpu.roll(value, shift, axis=1)


def kernel(
    sizes, edge,
    nb_ref, in_ref, x_out, r_out, len_out,
    ext, w_ext, r_ext, s_ext, geo, coef, chip_src, chip_dst, core_src, core_dst, dot_src, dot_dst,
    halo_send, halo_recv, dot_send, dot_recv,
):
    nx, ny, nz = sizes
    wide = edge + 4
    offsets = stencil()
    gx, gy, gz = lax.axis_index("gx"), lax.axis_index("gy"), lax.axis_index("gz")
    rank = (gx * ny + gy) * nz + gz

    def at(ox, oy, oz):
        return (lax.rem(gx + ox + nx, nx), lax.rem(gy + oy + ny, ny), lax.rem(gz + oz + nz, nz))

    others = [
        (a, b, c) for a in range(nx) for b in range(ny) for c in range(nz) if (a, b, c) != (0, 0, 0)
    ]
    others.sort(key=lambda o: -(min(o[0], nx - o[0]) + 2 * min(o[1], ny - o[1]) + 2 * min(o[2], nz - o[2])))

    barrier = pltpu.get_barrier_semaphore()
    for o in others:
        pl.semaphore_signal(barrier, inc=1, device_id=at(*o), device_id_type=MESH)

    lane = lax.broadcasted_iota(jnp.int32, (ROWS, LANES), 1)
    row = lax.broadcasted_iota(jnp.int32, (ROWS, LANES), 0)
    ye = lane // wide
    ze = lane - ye * wide
    y_low, y_high = ye < 2, (ye >= edge + 2) & (ye < wide)
    y_mid = (ye >= 2) & (ye < edge + 2)
    z_low, z_high = ze < 2, ze >= edge + 2
    z_mid = (ze >= 2) & (ze < edge + 2)
    src_zp = (ze >= edge) & z_mid
    src_zm = (ze < 4) & z_mid
    src_yp = (ye >= edge) & y_mid
    src_ym = (ye < 4) & y_mid

    def pack(planes, mask, base, step):
        out = None
        for c, plane in enumerate(planes):
            part = roll(jnp.where(mask, plane, 0.0), base + c * step)
            out = part if out is None else out + part
        return out

    def halo_copies(par, groups, comps):
        copies = []
        for oy in (-1, 1, 0):
            for oz in (-1, 1, 0):
                for ox in (1, 0):
                    if (ox, oy, oz) == (0, 0, 0):
                        continue
                    back = ox * 9 + (1 - oy) * 3 + 1 - oz
                    here = ox * 9 + (1 + oy) * 3 + 1 + oz
                    if oy == 0 and oz == 0:
                        src, dst = core_src.at[par, pl.ds(0, comps)], core_dst.at[par, pl.ds(0, comps)]
                    else:
                        kind = {1: 0, -1: 1}[oz] if oz else {1: 2, -1: 3}[oy]
                        src = chip_src.at[par, kind, pl.ds(0, groups)]
                        dst = chip_dst.at[par, back, pl.ds(0, groups)]
                    copies.append(
                        pltpu.make_async_remote_copy(
                            src_ref=src, dst_ref=dst,
                            send_sem=halo_send.at[par, here], recv_sem=halo_recv.at[par, back],
                            device_id=at(ox, oy, oz), device_id_type=MESH,
                        )
                    )
        return copies

    def halo_start(par, planes):
        parts = [planes] if len(planes) <= 4 else [planes[:4], planes[4:]]
        for g, part in enumerate(parts):
            chip_src[par, 0, g] = pack(part, src_zp, -edge, 2)
            chip_src[par, 1, g] = pack(part, src_zm, edge, -2)
            chip_src[par, 2, g] = pack(part, src_yp, -edge * wide, 2 * wide)
            chip_src[par, 3, g] = pack(part, src_ym, edge * wide, -2 * wide)
        for c, plane in enumerate(planes):
            core_src[par, c] = plane
        copies = halo_copies(par, len(parts), len(planes))
        for copy in copies:
            copy.start()
        return copies

    def halo_finish(par, planes, copies, target):
        for copy in copies:
            copy.wait_recv()
        parts = [planes] if len(planes) <= 4 else [planes[:4], planes[4:]]
        index = 0
        for g, part in enumerate(parts):
            merged = []
            for ox in (0, 1):
                def got(oy, oz):
                    return chip_dst[par, ox * 9 + (1 + oy) * 3 + 1 + oz, g]

                def column(oz):
                    near = got(0, oz)
                    low = roll(got(-1, oz), -edge * wide)
                    high = roll(got(1, oz), edge * wide)
                    return jnp.where(y_mid, near, jnp.where(y_low, low, high))

                merged.append((column(-1), column(1), got(-1, 0), got(1, 0)))
            for c, plane in enumerate(part):
                full = []
                for ox in (0, 1):
                    zl, zh, yl, yh = merged[ox]
                    base = plane if ox == 0 else core_dst[par, index]
                    base = jnp.where(y_low & z_mid, roll(yl, -2 * wide * c), base)
                    base = jnp.where(y_high & z_mid, roll(yh, 2 * wide * c), base)
                    base = jnp.where(z_low, roll(zl, -2 * c), base)
                    base = jnp.where(z_high, roll(zh, 2 * c), base)
                    full.append(jnp.where(ye < wide, base, 0.0))
                ref, k = target[index]
                ref[k, pl.ds(2, edge), :] = full[0][:edge]
                ref[k, pl.ds(0, 2), :] = full[1][edge - 2 : edge]
                ref[k, pl.ds(edge + 2, 2), :] = full[1][0:2]
                index += 1
        for copy in copies:
            copy.wait_send()

    inputs = [in_ref[c] for c in range(7)]
    live = (row < edge) & y_mid & z_mid & (ye < wide)
    jit, pol, field = inputs[0:3], jnp.where(live, inputs[3], 1.0), inputs[4:7]
    inv = 1.0 / pol
    x = [pol * f for f in field]
    ext[...] = jnp.zeros_like(ext)
    geo[...] = jnp.ones_like(geo)
    for ref in (w_ext, r_ext, s_ext):
        ref[...] = jnp.zeros_like(ref)

    pl.semaphore_wait(barrier, len(others))
    first = [*jit, pol, *x]
    copies = halo_start(0, first)

    home = row * (wide * wide) + lane + 2 * wide * wide
    hundred, ten = wide * wide, wide

    def slot(number, words):
        entry = nb_ref[number]
        rel = entry - home + (2 * hundred + hundred // 2)
        dx = (rel * 5243) >> 19
        rem = rel - dx * hundred - (hundred // 2 - 2 * ten - 5)
        dy = (rem * 6554) >> 16
        dz = rem - dy * ten - 3
        bit = jnp.where(entry >= 0, jnp.left_shift(1, jnp.clip(dy * 5 + dz, 0, 24)), 0)
        return tuple(word | jnp.where(dx == k, bit, 0) for k, word in enumerate(words))

    zero = jnp.zeros((ROWS, LANES), jnp.int32)
    words = lax.fori_loop(0, nb_ref.shape[0], slot, (zero,) * 5)

    halo_finish(0, first, copies, [(geo, 0), (geo, 1), (geo, 2), (geo, 3), (ext, 0), (ext, 1), (ext, 2)])

    for n, d in enumerate(offsets):
        shift = -(d[1] * wide + d[2])
        bit = 5 * (d[1] + 2) + d[2] + 2
        present = (words[d[0] + 2] & (1 << bit)) != 0
        near = [roll(geo[k, pl.ds(d[0] + 2, ROWS), :], shift) for k in range(4)]
        sep = [
            jnp.where(present, (d[k] + near[k] - jit[k]) * site_spacing, site_spacing) for k in range(3)
        ]
        sq = sep[0] * sep[0] + sep[1] * sep[1] + sep[2] * sep[2]
        dist = jnp.sqrt(sq)
        cube = sq * dist
        damp = thole_damping * cube / jnp.sqrt(pol * near[3])
        fall = jnp.exp(-damp)
        iso = jnp.where(present, (1.0 - fall) / cube, 0.0)
        rad = jnp.where(present, 3.0 * (1.0 - (1.0 + damp) * fall) / (cube * sq), 0.0)
        rs = [rad * s for s in sep]
        coef[n, 0] = rs[0] * sep[0] - iso
        coef[n, 1] = rs[0] * sep[1]
        coef[n, 2] = rs[0] * sep[2]
        coef[n, 3] = rs[1] * sep[1] - iso
        coef[n, 4] = rs[1] * sep[2]
        coef[n, 5] = rs[2] * sep[2] - iso

    def operate(planes):
        acc = [[None] * 5 for _ in range(3)]
        for n, d in enumerate(offsets):
            shift = -(d[1] * wide + d[2])
            a, b, c = [roll(ext[k, pl.ds(d[0] + 2, ROWS), :], shift) for k in range(3)]
            xx, xy, xz, yy, yz, zz = [coef[n, k] for k in range(6)]
            for k, term in enumerate(
                (xx * a + xy * b + xz * c, xy * a + yy * b + yz * c, xz * a + yz * b + zz * c)
            ):
                old = acc[k][d[0] + 2]
                acc[k][d[0] + 2] = term if old is None else old + term
        return [
            planes[k] * inv - (((acc[k][0] + acc[k][1]) + (acc[k][3] + acc[k][4])) + acc[k][2])
            for k in range(3)
        ]

    image = operate(x)
    r = [jnp.where(live, field[k] - image[k], 0.0) for k in range(3)]
    u = [pol * v for v in r]
    copies = halo_start(1, r)
    halo_finish(1, r, copies, [(r_ext, 0), (r_ext, 1), (r_ext, 2)])
    for k in range(3):
        ext[k] = geo[3] * r_ext[k]
    w = operate(u)

    pick = lax.broadcasted_iota(jnp.int32, (1, LANES), 1)

    def dot_copies(par):
        return [
            pltpu.make_async_remote_copy(
                src_ref=dot_src.at[par], dst_ref=dot_dst.at[par, rank],
                send_sem=dot_send.at[par, k], recv_sem=dot_recv.at[par, k],
                device_id=at(*o), device_id_type=MESH,
            )
            for k, o in enumerate(others)
        ]

    def total(value):
        return jnp.sum(jnp.sum(value, axis=0, keepdims=True), axis=1, keepdims=True)

    def dots_start(par, r, u, w):
        gamma = total(r[0] * u[0] + r[1] * u[1] + r[2] * u[2])
        delta = total(w[0] * u[0] + w[1] * u[1] + w[2] * u[2])
        line = jnp.where(pick == 0, gamma, jnp.where(pick == 1, delta, 0.0))
        dot_src[par] = line
        dot_dst[par, rank] = line
        copies = dot_copies(par)
        for copy in copies:
            copy.start()
        return copies

    def dots_finish(par, copies):
        for copy in copies:
            copy.wait_recv()
        line = jnp.sum(dot_dst[par, :, 0, :], axis=0, keepdims=True)
        for copy in copies:
            copy.wait_send()
        gamma = jnp.sum(jnp.where(pick == 0, line, 0.0), axis=1, keepdims=True)
        delta = jnp.sum(jnp.where(pick == 1, line, 0.0), axis=1, keepdims=True)
        return gamma, delta

    def lengths(number, gamma, delta, gamma_old, step_old):
        beta = gamma / gamma_old
        step = gamma / (delta - beta * gamma / step_old)
        len_out[pl.ds(number, 1), :] = jnp.broadcast_to(step, (1, LANES))
        return beta, step

    def axpy(a, s, b):
        return [a[k] + s * b[k] for k in range(3)]

    def iteration(number, state):
        x, r, u, w, p, s, gamma_old, step_old = state
        par = lax.rem(number, 2)
        dots = dots_start(par, r, u, w)
        halos = halo_start(par, w)
        halo_finish(par, w, halos, [(w_ext, 0), (w_ext, 1), (w_ext, 2)])
        gamma, delta = dots_finish(par, dots)
        beta, step = lengths(number, gamma, delta, gamma_old, step_old)
        for k in range(3):
            s_new = w_ext[k] + beta * s_ext[k]
            r_new = r_ext[k] - step * s_new
            s_ext[k] = s_new
            r_ext[k] = r_new
            ext[k] = geo[3] * r_new
        s, p = axpy(w, beta, s), axpy(u, beta, p)
        x, r = axpy(x, step, p), axpy(r, -step, s)
        u = [pol * v for v in r]
        w = operate(u)
        return x, r, u, w, p, s, gamma, step

    none = [jnp.zeros((ROWS, LANES), jnp.float32)] * 3
    far = jnp.full((1, 1), jnp.inf, jnp.float32)
    one = jnp.ones((1, 1), jnp.float32)
    state = (x, r, u, w, none, none, far, one)
    x, r, u, w, p, s, gamma_old, step_old = lax.fori_loop(0, ITERS - 1, iteration, state)
    last = (ITERS - 1) % 2
    dots = dots_start(last, r, u, w)
    gamma, delta = dots_finish(last, dots)
    beta, step = lengths(ITERS - 1, gamma, delta, gamma_old, step_old)
    p, s = axpy(u, beta, p), axpy(w, beta, s)
    x, r = axpy(x, step, p), axpy(r, -step, s)
    for k in range(3):
        x_out[k] = x[k]
        r_out[k] = r[k]


def solution(mesh):
    sizes = tuple(mesh.shape[a] for a in ("gx", "gy", "gz"))
    assert sizes[0] == 2
    count = sizes[0] * sizes[1] * sizes[2]

    def local(permanent_field, polar, jitter, neighbors):
        edge = polar.shape[0]
        wide = edge + 4
        slots = neighbors.shape[-1]

        def spread(array, fill):
            array = jnp.moveaxis(array, -1, 0)
            array = jnp.pad(array, ((0, 0), (0, ROWS - edge), (2, 2), (2, 2)), constant_values=fill)
            array = array.reshape(array.shape[0], ROWS, wide * wide)
            return jnp.pad(array, ((0, 0), (0, 0), (0, LANES - wide * wide)), constant_values=fill)

        bundle = jnp.concatenate([jitter, polar[..., None], permanent_field], axis=-1)
        bundle = spread(bundle, 0.0)
        plane = jax.ShapeDtypeStruct((3, ROWS, LANES), jnp.float32)
        vmem = pl.BlockSpec(memory_space=pltpu.VMEM)
        f32 = jnp.float32
        x, r, steps = pl.pallas_call(
            functools.partial(kernel, sizes, edge),
            out_shape=(plane, plane, jax.ShapeDtypeStruct((ITERS, LANES), f32)),
            in_specs=[vmem, vmem],
            out_specs=(vmem, vmem, vmem),
            scratch_shapes=[
                *[pltpu.VMEM((3, 16, LANES), f32)] * 4,
                pltpu.VMEM((4, 16, LANES), f32),
                pltpu.VMEM((len(stencil()), 6, ROWS, LANES), f32),
                pltpu.VMEM((2, 4, 2, ROWS, LANES), f32),
                pltpu.VMEM((2, 18, 2, ROWS, LANES), f32),
                pltpu.VMEM((2, 7, ROWS, LANES), f32),
                pltpu.VMEM((2, 7, ROWS, LANES), f32),
                pltpu.VMEM((2, 1, LANES), f32),
                pltpu.VMEM((2, count, 1, LANES), f32),
                pltpu.SemaphoreType.DMA((2, 18)),
                pltpu.SemaphoreType.DMA((2, 18)),
                pltpu.SemaphoreType.DMA((2, count)),
                pltpu.SemaphoreType.DMA((2, count)),
            ],
            compiler_params=pltpu.CompilerParams(collective_id=0, has_side_effects=True),
        )(spread(neighbors, -1), bundle)

        def gather(planes):
            planes = planes[:, :edge, : wide * wide].reshape(3, edge, wide, wide)
            return jnp.moveaxis(planes[:, :, 2:-2, 2:-2], 0, -1)

        return gather(x), gather(r), steps[:, 0]

    return jax.shard_map(
        local,
        mesh=mesh,
        in_specs=(
            P("gx", "gy", "gz", None),
            P("gx", "gy", "gz"),
            P("gx", "gy", "gz", None),
            P("gx", "gy", "gz", None),
        ),
        out_specs=(P("gx", "gy", "gz", None), P("gx", "gy", "gz", None), P()),
        check_vma=False,
    )
```

time: 862 us -> 74.7 us (0.09)
  blocking collectives: 321 us -> 0 us
  local copies, waits for them, and re-layouts: 307 us -> 6.6 us
  waiting for transfers between devices: 107 us -> 0 us
  starting transfers between devices: 80.1 us -> 0 us
  Pallas kernels: 0 us -> 66 us
  between operations: 31.3 us -> 0.73 us
  other arithmetic: 14.7 us -> 0.99 us
    psum x8 -> x0, blocking collectives: 321 us -> none  [joined(): lax.psum((jnp.sum(left_vec * right_vec), jnp.sum(right_vec * other_vec)),...]
    gather x19 -> x0, local copies, waits for them, and re-layouts: 276 us -> none  [the longest x18 253 us: operate(): values = ghosts.reshape(padded_count, 3)[clipped]]
    ppermute x60 -> x0, waiting for transfers between devices: 107 us -> none  [the longest x30 78.6 us: padded_2(): lax.ppermute(tail, axis, [(i, (i + 1) % count) for i in range(ends)])]
    ppermute x60 -> x0, starting transfers between devices: 80.1 us -> none  [the longest x30 47.3 us: padded_2(): lax.ppermute(head, axis, [((i + 1) % count, i) for i in range(ends)])]
    pallas_call x0 -> x1, Pallas kernels: none -> 66 us  [local(): pl.pallas_call(functools.partial(kernel, sizes, edge), out_shape=(plane,...]
    unnamed x13 -> x10, local copies, waits for them, and re-layouts: 11.9 us -> 2.3 us
    slice x38 -> x1, local copies, waits for them, and re-layouts: 10.4 us -> 1.31 us  [local(): return (gather(x), gather(r), steps[:, 0])]
  transfers between devices with their start and end apart: 60 -> 0, of which waited for: 50 -> 0; matrix products, arithmetic and copies ran while one was open for 4% -> 0% of each run, Pallas kernels for 0% -> 0%
where the time goes in v1:
time: 74.7 us; the launch traced here: 74.3 us
  Pallas kernels  66 us (88%)
  local copies, waits for them, and re-layouts  6.6 us (9%)
  other arithmetic  0.99 us (1%)
    pallas_call x1, Pallas kernels, local(): pl.pallas_call(functools.partial(kernel, sizes, edge), out_shape=(plane,...  66 us
    unnamed x10, local copies, waits for them, and re-layouts  2.3 us

profile of v1, /device:TPU:0, one launch (start us, length us, event | category | flops | bytes accessed | tf_op | source)
XLA Modules:
  0.0 74.3 jit_solution(1069790344773010570)
XLA Ops:
  0.6 0.8 %copy.13 = f32[6,6,6,1]{2,3,1,0:T(1,128)S(1)} copy(f32[6,6,6,1]{2,1,0,3:T(8,128)} %bitcast.13) | data formatting | bytes 1728 | tf_op jit(solution)/shard_map/broadcast_in_dim | solution.py:327
  1.4 1.0 %maximum_bitcast_fusion = f32[7,6,6,6]{3,0,2,1:T(8,128)S(1)} fusion(f32[6,6,6,3]{2,3,1,0:T(4,128)} %param.4, f32[6,6,6,1]{2,3,1,0:T(1,128)S(1)} %copy.13, f32[6,6,6,3]{2,3,1,0:T(4,128)} %param.6), kind=kLoop, calls=%fused_computation | loop fusion | flops 3024 | bytes 12096 | tf_op jit(solution)/shard_map/transpose | solution.py:322
  2.4 0.0 copy-start
  2.4 0.9 %copy-done = s32[6,6,6,56]{3,2,1,0:T(8,128)S(1)} copy-done((s32[6,6,6,56]{3,2,1,0:T(8,128)S(1)}, s32[6,6,6,56]{3,2,1,0:T(8,128)}, u32[]{:S(2)}) %copy-start) | copy-done | bytes 48408
  3.4 0.2 copy.12
  3.6 0.7 pad.17.nb_ref
  4.3 0.2 pad.18.clone
  4.5 0.2 reshape.19
  4.6 0.6 pad.19.in_ref
  5.2 66.0 %shard_map.67 = (f32[3,8,128]{2,1,0:T(8,128)}, f32[3,8,128]{2,1,0:T(8,128)}, f32[8,128]{1,0:T(8,128)}) custom-call(s32[56,8,128]{2,1,0:T(8,128)} %pad.17.nb_ref, f32[7,8,128]{2,1,0:T(8,128)} %pad.19.in_ref), custom_call_target="tpu_custom_call" | custom-call | tf_op jit(solution)/shard_map/pallas_call | solution.py:332
  71.2 0.0 copy-start.2
  71.2 1.3 %slice_reduce_fusion = f32[8]{0:T(128)} fusion(f32[8,128]{1,0:T(8,128)} %get-tuple-element.8), kind=kLoop, calls=%fused_computation.3 | loop fusion | bytes 64 | tf_op jit(solution)/shard_map/slice | solution.py:359
  72.5 0.0 copy-done.2
  72.5 0.1 reshape.21
  72.6 0.1 slice_bitcast_fusion
  72.7 0.0 copy-start.1
  72.7 0.7 copy.16
  73.4 0.0 copy-done.1
  73.4 0.1 reshape.20
  73.5 0.1 slice_bitcast_fusion.1
  73.6 0.7 copy.15
  (3 shorter events, 0.1 us)
Async XLA Ops:
  2.4 0.9 %copy-start = (s32[6,6,6,56]{3,2,1,0:T(8,128)S(1)}, s32[6,6,6,56]{3,2,1,0:T(8,128)}, u32[]{:S(2)}) copy-start(s32[6,6,6,56]{3,2,1,0:T(8,128)} %param.7) | copy-start | bytes 145156
  71.2 1.3 %copy-start.2 = (f32[3,8,128]{2,1,0:T(8,128)S(1)}, f32[3,8,128]{2,1,0:T(8,128)}, u32[]{:S(2)}) copy-start(f32[3,8,128]{2,1,0:T(8,128)} %get-tuple-element.7) | copy-start | bytes 36868
  72.7 0.7 copy-start.1

commit v2 on v1

--- a/solution.py
+++ b/solution.py
@@ -97,7 +97,7 @@
                     )
         return copies
 
-    def halo_start(par, planes):
+    def halo_pack(par, planes):
         parts = [planes] if len(planes) <= 4 else [planes[:4], planes[4:]]
         for g, part in enumerate(parts):
             chip_src[par, 0, g] = pack(part, src_zp, -edge, 2)
@@ -106,7 +106,9 @@
             chip_src[par, 3, g] = pack(part, src_ym, edge * wide, -2 * wide)
         for c, plane in enumerate(planes):
             core_src[par, c] = plane
-        copies = halo_copies(par, len(parts), len(planes))
+
+    def halo_start(par, planes):
+        copies = halo_copies(par, 1 if len(planes) <= 4 else 2, len(planes))
         for copy in copies:
             copy.start()
         return copies
@@ -153,12 +155,14 @@
     inv = 1.0 / pol
     x = [pol * f for f in field]
     ext[...] = jnp.zeros_like(ext)
+    len_out[...] = jnp.zeros_like(len_out)
     geo[...] = jnp.ones_like(geo)
     for ref in (w_ext, r_ext, s_ext):
         ref[...] = jnp.zeros_like(ref)
 
+    first = [*jit, pol, *x]
+    halo_pack(0, first)
     pl.semaphore_wait(barrier, len(others))
-    first = [*jit, pol, *x]
     copies = halo_start(0, first)
 
     home = row * (wide * wide) + lane + 2 * wide * wide
@@ -221,6 +225,7 @@
     image = operate(x)
     r = [jnp.where(live, field[k] - image[k], 0.0) for k in range(3)]
     u = [pol * v for v in r]
+    halo_pack(1, r)
     copies = halo_start(1, r)
     halo_finish(1, r, copies, [(r_ext, 0), (r_ext, 1), (r_ext, 2)])
     for k in range(3):
@@ -255,10 +260,10 @@
 
     def dots_finish(par, copies):
         for copy in copies:
+            copy.wait_send()
+        for copy in copies:
             copy.wait_recv()
         line = jnp.sum(dot_dst[par, :, 0, :], axis=0, keepdims=True)
-        for copy in copies:
-            copy.wait_send()
         gamma = jnp.sum(jnp.where(pick == 0, line, 0.0), axis=1, keepdims=True)
         delta = jnp.sum(jnp.where(pick == 1, line, 0.0), axis=1, keepdims=True)
         return gamma, delta
@@ -266,7 +271,7 @@
     def lengths(number, gamma, delta, gamma_old, step_old):
         beta = gamma / gamma_old
         step = gamma / (delta - beta * gamma / step_old)
-        len_out[pl.ds(number, 1), :] = jnp.broadcast_to(step, (1, LANES))
+        len_out[...] = jnp.where(pick == number, step, len_out[...])
         return beta, step
 
     def axpy(a, s, b):
@@ -275,6 +280,7 @@
     def iteration(number, state):
         x, r, u, w, p, s, gamma_old, step_old = state
         par = lax.rem(number, 2)
+        halo_pack(par, w)
         dots = dots_start(par, r, u, w)
         halos = halo_start(par, w)
         halo_finish(par, w, halos, [(w_ext, 0), (w_ext, 1), (w_ext, 2)])
@@ -331,7 +337,7 @@
         f32 = jnp.float32
         x, r, steps = pl.pallas_call(
             functools.partial(kernel, sizes, edge),
-            out_shape=(plane, plane, jax.ShapeDtypeStruct((ITERS, LANES), f32)),
+            out_shape=(plane, plane, jax.ShapeDtypeStruct((1, LANES), f32)),
             in_specs=[vmem, vmem],
             out_specs=(vmem, vmem, vmem),
             scratch_shapes=[
@@ -356,7 +362,7 @@
             planes = planes[:, :edge, : wide * wide].reshape(3, edge, wide, wide)
             return jnp.moveaxis(planes[:, :, 2:-2, 2:-2], 0, -1)
 
-        return gather(x), gather(r), steps[:, 0]
+        return gather(x), gather(r), steps[0, :ITERS]
 
     return jax.shard_map(
         local,

time: 74.7 us -> 75.2 us (level)
    slice x1 -> x0, local copies, waits for them, and re-layouts: 1.31 us -> none  [local(): return (gather(x), gather(r), steps[:, 0])]
where the time goes in v2:
time: 75.2 us; the launch traced here: 74.8 us
  Pallas kernels  65.9 us (88%)
  local copies, waits for them, and re-layouts  7.17 us (10%)
  other arithmetic  0.99 us (1%)
    pallas_call x1, Pallas kernels, local(): pl.pallas_call(functools.partial(kernel, sizes, edge), out_shape=(plane,...  65.9 us
    unnamed x10, local copies, waits for them, and re-layouts  2.96 us

profile of v2, /device:TPU:0, one launch (start us, length us, event | category | flops | bytes accessed | tf_op | source)
XLA Modules:
  0.0 74.8 jit_solution(16891563131730063988)
XLA Ops:
  0.6 0.8 %copy.13 = f32[6,6,6,1]{2,3,1,0:T(1,128)S(1)} copy(f32[6,6,6,1]{2,1,0,3:T(8,128)} %bitcast.15) | data formatting | bytes 1728 | tf_op jit(solution)/shard_map/broadcast_in_dim | solution.py:333
  1.4 1.0 %maximum_bitcast_fusion = f32[7,6,6,6]{3,0,2,1:T(8,128)S(1)} fusion(f32[6,6,6,3]{2,3,1,0:T(4,128)} %param.4, f32[6,6,6,1]{2,3,1,0:T(1,128)S(1)} %copy.13, f32[6,6,6,3]{2,3,1,0:T(4,128)} %param.6), kind=kLoop, calls=%fused_computation | loop fusion | flops 3024 | bytes 12096 | tf_op jit(solution)/shard_map/transpose | solution.py:328
  2.4 0.0 copy-start
  2.4 0.9 %copy-done = s32[6,6,6,56]{3,2,1,0:T(8,128)S(1)} copy-done((s32[6,6,6,56]{3,2,1,0:T(8,128)S(1)}, s32[6,6,6,56]{3,2,1,0:T(8,128)}, u32[]{:S(2)}) %copy-start) | copy-done | bytes 48408
  3.4 0.2 copy.12
  3.6 0.7 pad.17.nb_ref
  4.3 0.2 pad.18.clone
  4.5 0.2 reshape.19
  4.6 0.6 pad.19.in_ref
  5.2 65.9 %shard_map.67 = (f32[3,8,128]{2,1,0:T(8,128)}, f32[3,8,128]{2,1,0:T(8,128)}, f32[1,128]{1,0:T(1,128)}) custom-call(s32[56,8,128]{2,1,0:T(8,128)} %pad.17.nb_ref, f32[7,8,128]{2,1,0:T(8,128)} %pad.19.in_ref), custom_call_target="tpu_custom_call" | custom-call | tf_op jit(solution)/shard_map/pallas_call | solution.py:338
  71.2 0.0 copy-start.2
  71.2 0.7 copy-done.2
  71.8 0.5 slice_bitcast_fusion.2
  72.4 0.8 %reshape.21 = f32[3,6,10,10]{3,2,1,0:T(8,128)S(1)} reshape(f32[3,6,100]{2,1,0:T(8,128)} %bitcast.17) | data formatting | bytes 14400 | tf_op jit(solution)/shard_map/reshape | solution.py:362
  73.2 0.1 slice_bitcast_fusion
  73.2 0.0 copy-start.1
  73.3 0.7 copy.16
  73.9 0.0 copy-done.1
  74.0 0.1 reshape.20
  74.1 0.1 slice_bitcast_fusion.1
  74.2 0.7 copy.15
  (3 shorter events, 0.1 us)
Async XLA Ops:
  2.4 0.9 %copy-start = (s32[6,6,6,56]{3,2,1,0:T(8,128)S(1)}, s32[6,6,6,56]{3,2,1,0:T(8,128)}, u32[]{:S(2)}) copy-start(s32[6,6,6,56]{3,2,1,0:T(8,128)} %param.7) | copy-start | bytes 145156
  71.2 0.7 copy-start.2
  73.2 0.7 copy-start.1
